TPU v7x, 32 devices: a whole 2x2x4 slice. The times are simulated.
32 devices in a mesh: wa: 4 (over z), bl: 8 (over y, x, core).
Axes of the slice: x: 2, y: 2, z: 4, core: 2. Of those that a mesh axis runs over, the one named last changes fastest.
Arguments:
- visibilities: float32 [4, 16, 2, 128], P('wa', 'bl'), may hold values from -6 to 6
- weights: float32 [4, 16, 128], P('wa', 'bl'), may hold values from 0.25 to 4
- cell_index: int32 [4, 16, 128], P('wa', 'bl'), may hold values from 0 to 1048575
- kernel_index: int32 [4, 16, 128], P('wa', 'bl'), may hold values from 0 to 255
- layer_index: int32 [4, 16, 128], P('wa', 'bl'), may hold values from 0 to 1
- tile_counts: int32 [4, 16], P('wa', 'bl'), may hold values from 1 to 128
- kernel_table: float32 [16, 8], replicated, may hold values from 0.05 to 0.3
- layer_depth: float32 [8], P('wa'), may hold values from -150 to 150
Outputs:
- image: float32 [1024, 1024], P('wa', 'bl')
All inputs are finite; a program needn't handle non-finite values.
Results may differ from a plain program's by a relative error of at most 0.0003.
Values sent between devices are 32-bit elements; how exact they have to be, the bound alone decides.
No kernel may reach another device: no remote copies, remote signals or barrier semaphores. Data moves between devices by JAX's collectives and lax.ppermute only.
A program may use at most 128 MiB of HBM per device.

v0:
```python
import functools
import math

import jax
import jax.numpy as jnp
from jax import lax
from jax.experimental import pallas as pl
from jax.experimental.pallas import tpu as pltpu
from jax.sharding import PartitionSpec as P

GRID = 1024
SUPPORT = 8
OVERSAMPLE = 16
FIELD_OF_VIEW = 0.6

LANES = 128
LOW = LANES // OVERSAMPLE
FIELDS = 4
LONG = 4
SENT = 2

highest = lax.Precision.HIGHEST
last_dims = (((1,), (1,)), ((), ()))

COS_TERMS = (0.2196967899799347, -1.3318802118301392, 4.058412075042725, -4.934792995452881, 0.9999999403953552)
SIN_TERMS = (0.0772201269865036, -0.5980451703071594, 2.5500314235687256, -5.1677069664001465, 3.141592502593994)
GRID_BITS = GRID.bit_length() - 1
LOW_BITS = LOW.bit_length() - 1
POSITION_BITS = OVERSAMPLE.bit_length() - 1


def iota(shape, dim):
    return lax.broadcasted_iota(jnp.int32, shape, dim)


def half_turn(value):
    square = value * value
    cosine = jnp.full_like(square, COS_TERMS[0])
    for term in COS_TERMS[1:]:
        cosine = cosine * square + term
    sine = jnp.full_like(square, SIN_TERMS[0])
    for term in SIN_TERMS[1:]:
        sine = sine * square + term
    return cosine, sine * value


def unit_root(power):
    moved = power + GRID // 4
    step = (moved & (GRID // 2 - 1)) - GRID // 4
    cosine, sine = half_turn(step.astype(jnp.float32) * (2.0 / GRID))
    flip = (moved & (GRID // 2)) != 0
    return jnp.where(flip, -cosine, cosine), jnp.where(flip, -sine, sine)


def split_two(value):
    upper = value.astype(jnp.bfloat16)
    return upper, (value - upper.astype(jnp.float32)).astype(jnp.bfloat16)


def pack_kernel(layer_dev, count_ref, depth_ref, vis_ref, weight_ref, cell_ref, kernel_ref, layer_ref, out_ref):
    tiles, samples = weight_ref.shape
    slots = tiles * samples
    lane = iota((1, samples), 1)
    rows = []
    used_weight = []
    for tile in range(tiles):
        used = lane < count_ref[0, tile]
        used_weight.append(jnp.where(used, weight_ref[tile : tile + 1, :], 0.0))
        for layer in range(layer_dev):
            rows.append(jnp.where(used & (layer_ref[tile : tile + 1, :] == layer), 1.0, 0.0))
    mask = jnp.concatenate(rows, axis=0)
    upper = jnp.where(iota((samples, samples), 0) <= iota((samples, samples), 1), 1.0, 0.0)
    rank = jnp.dot(
        mask.astype(jnp.bfloat16), upper.astype(jnp.bfloat16), preferred_element_type=jnp.float32
    )
    total = jnp.sum(mask, axis=1, keepdims=True)
    base = jnp.zeros((1, 1), jnp.float32)
    layer_count = []
    target = [jnp.full((1, samples), -1.0, jnp.float32) for tile in range(tiles)]
    for layer in range(layer_dev):
        start = base
        for tile in range(tiles):
            row = tile * layer_dev + layer
            place = base + rank[row : row + 1, :] - 1.0
            target[tile] = jnp.where(mask[row : row + 1, :] > 0.0, place, target[tile])
            base = base + total[row : row + 1, :]
        layer_count.append(base - start)
    target = jnp.concatenate(target, axis=1).astype(jnp.int32)
    chosen = jnp.where(iota((slots, slots), 0) == target, 1.0, 0.0).astype(jnp.bfloat16)
    weight_row = jnp.concatenate(used_weight, axis=1)
    real_row = jnp.concatenate([vis_ref[2 * t : 2 * t + 1, :] for t in range(tiles)], axis=1)
    imag_row = jnp.concatenate([vis_ref[2 * t + 1 : 2 * t + 2, :] for t in range(tiles)], axis=1)
    cell_row = jnp.concatenate([cell_ref[t : t + 1, :] for t in range(tiles)], axis=1)
    kernel_row = jnp.concatenate([kernel_ref[t : t + 1, :] for t in range(tiles)], axis=1)
    fields = jnp.concatenate(
        [
            real_row * weight_row,
            imag_row * weight_row,
            cell_row.astype(jnp.float32),
            kernel_row.astype(jnp.float32),
        ],
        axis=0,
    )
    parts = []
    for part in range(3):
        upper_part = fields.astype(jnp.bfloat16)
        parts.append(upper_part.astype(jnp.float32))
        fields = fields - upper_part.astype(jnp.float32)
    moved = lax.dot_general(
        jnp.concatenate(parts, axis=0).astype(jnp.bfloat16),
        chosen,
        last_dims,
        preferred_element_type=jnp.float32,
    )
    moved = moved[:FIELDS] + moved[FIELDS : 2 * FIELDS] + moved[2 * FIELDS :]
    wide = iota((SENT, LANES), 1)
    extra = jnp.zeros((SENT, LANES), jnp.float32)
    square = jnp.sum(weight_row * weight_row, axis=1, keepdims=True)
    extra = jnp.where(wide == 2 * layer_dev, square, extra)
    for layer in range(layer_dev):
        extra = jnp.where(wide == layer, layer_count[layer], extra)
        extra = jnp.where(wide == layer_dev + layer, depth_ref[layer], extra)
    for device in range(out_ref.shape[0]):
        for pair in range(FIELDS // SENT):
            out_ref[device, :, pair * slots : (pair + 1) * slots] = moved[SENT * pair : SENT * (pair + 1)]
        out_ref[device, :, FIELDS // SENT * slots :] = extra


def table_kernel(taps_ref, first_u, base_u, step_u, first_v, base_v, step_v, depth_ref):
    rows, columns = depth_ref.shape
    row_start = lax.axis_index("wa") * rows
    column_start = lax.axis_index("bl") * (GRID // lax.axis_size("bl"))
    low_lane = iota((OVERSAMPLE, LANES), 1) & (LOW - 1)
    position_lane = iota((OVERSAMPLE, LANES), 1) >> LOW_BITS
    picked = jnp.where(position_lane == iota((OVERSAMPLE, LANES), 0), 1.0, 0.0)
    taps = jnp.dot(taps_ref[...], picked, precision=highest, preferred_element_type=jnp.float32)
    band = jnp.zeros((OVERSAMPLE, LANES), jnp.float32)
    for tap in range(SUPPORT):
        band = jnp.where(iota((OVERSAMPLE, LANES), 0) - low_lane == tap, taps[tap : tap + 1, :], band)

    def fill(first, base, step, start):
        count = first.shape[1]
        pixel = start + iota((count, OVERSAMPLE), 0)
        roots = unit_root((iota((count, OVERSAMPLE), 1) - SUPPORT // 2) * pixel)
        for part in range(2):
            first[part] = jnp.dot(roots[part], band, precision=highest, preferred_element_type=jnp.float32)
        roots = unit_root(iota((8, LANES), 1) * LOW * (start + iota((8, LANES), 0)))
        for part in range(2):
            base[part] = roots[part]
        count = step.shape[1]
        roots = unit_root(iota((count, LANES), 1) * LOW * 8 * iota((count, LANES), 0))
        for part in range(2):
            step[part] = roots[part]

    fill(first_u, base_u, step_u, row_start)
    fill(first_v, base_v, step_v, column_start)
    pixel_size = FIELD_OF_VIEW / GRID
    x_coord = (row_start + iota((rows, columns), 0) - GRID // 2).astype(jnp.float32) * pixel_size
    y_coord = (column_start + iota((rows, columns), 1) - GRID // 2).astype(jnp.float32) * pixel_size
    depth_ref[...] = jnp.sqrt(jnp.maximum(1.0 - x_coord * x_coord - y_coord * y_coord, 0.0)) - 1.0


def image_kernel(
    layer_dev,
    groups,
    members,
    slot_ref,
    first_u,
    base_u,
    step_u,
    first_v,
    base_v,
    step_v,
    depth_ref,
    out_ref,
    extra_ref,
    stream_ref,
    index_refs,
    wave_refs,
    left_refs,
    right_refs,
    sum_ref,
    start_ref,
    count_ref,
    copy_sem,
):
    rows, columns = out_ref.shape
    wide = first_v.shape[1]
    slots = (slot_ref.shape[2] - LANES) * SENT // FIELDS
    counts_at = slot_ref.shape[2] - LANES
    source_tiles = slots // LANES
    regions = groups * layer_dev
    region_tiles = stream_ref.shape[0] // regions

    copy = pltpu.make_async_copy(slot_ref.at[:, pl.ds(0, 1), pl.ds(counts_at, LANES)], extra_ref, copy_sem)
    copy.start()
    sum_ref[...] = jnp.zeros_like(sum_ref)

    lane = iota((FIELDS, LANES), 1)

    def join(group, filled_tiles):
        base = [0] * layer_dev
        for member in range(members):
            device = group * members + member
            source = []
            for t in range(source_tiles):
                pieces = [
                    slot_ref[device, :, slots * pair + LANES * t : slots * pair + LANES * (t + 1)]
                    for pair in range(FIELDS // SENT)
                ]
                source.append(jnp.concatenate(pieces, axis=0))
            origin = 0
            for layer in range(layer_dev):
                count = slot_ref[device, 0, counts_at + layer].astype(jnp.int32)
                offset = base[layer] - origin
                shift = offset & (LANES - 1)
                tile = offset >> 7
                turned = [pltpu.roll(part, shift, 1) for part in source]
                region = (group * layer_dev + layer) * region_tiles + source_tiles
                for t in range(source_tiles + 1):
                    if t == 0:
                        value = turned[0]
                    elif t == source_tiles:
                        value = turned[t - 1]
                    else:
                        value = jnp.where(lane >= shift, turned[t], turned[t - 1])
                    where = region + tile + t
                    keep = lane < base[layer] - (tile + t) * LANES
                    stream_ref[where] = jnp.where(keep, stream_ref[where], value)
                base[layer] = base[layer] + count
                origin = origin + count
        for layer in range(layer_dev):
            region = group * layer_dev + layer
            start_ref[region] = filled_tiles
            count_ref[region] = base[layer]
            filled_tiles = filled_tiles + ((base[layer] + LANES - 1) >> 7)
        return filled_tiles

    tile_total = 0
    for group in range(groups):
        tile_total = join(group, tile_total)

    def find(tile):
        region = 0
        for other in range(1, regions):
            region = region + jnp.where(tile >= start_ref[other], 1, 0)
        first = start_ref[region]
        valid = jnp.where(tile < tile_total, count_ref[region] - (tile - first) * LANES, 0)
        place = jnp.where(tile < tile_total, tile - first, 0)
        return region, region * region_tiles + source_tiles + place, valid

    steps_u, steps_v = step_u.shape[1], step_v.shape[1]

    def pick(ref, at, index):
        return [
            jnp.take_along_axis(ref[part, at : at + 8], index, axis=1, mode="promise_in_bounds") for part in range(2)
        ]

    def times(one, two):
        return one[0] * two[0] - one[1] * two[1], one[0] * two[1] + one[1] * two[0]

    def prepare(tile, parity, side):
        unused, place, valid = find(tile)
        content = stream_ref[place]
        live = iota((1, LANES), 1) < valid
        cell = jnp.where(live, content[2:3], 0.0).astype(jnp.int32)
        kernel = jnp.where(live, content[3:4], 0.0).astype(jnp.int32)
        row = cell >> GRID_BITS
        column = cell & (GRID - 1)
        index, wave = index_refs[parity][side], wave_refs[parity][side]
        index[0:1] = ((kernel >> POSITION_BITS) << LOW_BITS) + (row & (LOW - 1))
        index[1:2] = ((kernel & (OVERSAMPLE - 1)) << LOW_BITS) + (column & (LOW - 1))
        row_high = jnp.broadcast_to(row >> LOW_BITS, (8, LANES))
        column_high = jnp.broadcast_to(column >> LOW_BITS, (8, LANES))
        value = [jnp.broadcast_to(jnp.where(live, content[part : part + 1], 0.0), (8, LANES)) for part in range(2)]
        bases = (pick(base_u, 0, row_high), times(pick(base_v, 0, column_high), value))
        at = 0
        for base, step, high in zip(bases, (step_u, step_v), (row_high, column_high)):
            for part in range(2):
                wave[part, at : at + 8] = base[part]
            at = at + 8
            for block in range(0, step.shape[1], 8):
                picked = pick(step, block, high)
                for part in range(2):
                    wave[part, at : at + 8] = picked[part]
                at = at + 8

    def build(parity, side):
        left, right = left_refs[parity][side], right_refs[parity][side]
        wave = wave_refs[parity][side]
        row_index, column_index = [
            jnp.broadcast_to(index_refs[parity][side][k : k + 1], (8, LANES)) for k in range(2)
        ]
        row_base = [wave[part, 0:8] for part in range(2)]
        column_base = [wave[part, 8 + steps_u : 16 + steps_u] for part in range(2)]

        def turn(base, at):
            return times(base, [jnp.broadcast_to(wave[part, at : at + 1], (8, LANES)) for part in range(2)])

        def paired(low, high):
            return [split_two(jnp.concatenate([low[part], high[part]], axis=0)) for part in range(2)]

        period = 8 * steps_u
        for at in range(0, period, 16):
            second = [turn(row_base, 8 + (at + half) // 8) for half in (0, 8)]
            for again in range(at, rows, period):
                both = paired(*[times(pick(first_u, again + 8 * k, row_index), second[k]) for k in range(2)])
                for part in range(2):
                    for level in range(2):
                        left[level, part, again : again + 16] = both[part][level]
        for at in range(0, wide, 16):
            second = [turn(column_base, 16 + steps_u + (at + half) // 8) for half in (0, 8)]
            both = paired(*[times(pick(first_v, at + 8 * k, column_index), second[k]) for k in range(2)])
            for level in range(2):
                right[level, 0, at : at + 16] = both[0][level]
                right[level, 1, at : at + 16] = -both[1][level]
                right[level, 0, wide + at : wide + at + 16] = both[1][level]
                right[level, 1, wide + at : wide + at + 16] = both[0][level]

    def add(tile, parity, side):
        left, right = left_refs[parity][side], right_refs[parity][side]
        owner = find(tile)[0]
        product = lax.dot_general(
            jnp.concatenate([left[level, part] for level in (0, 1, 0) for part in range(2)], axis=1),
            jnp.concatenate([right[level, part] for level in (0, 0, 1) for part in range(2)], axis=1),
            last_dims,
            preferred_element_type=jnp.float32,
        )
        sum_ref[owner] = sum_ref[owner] + product

    for side in range(2):
        prepare(side, 0, side)
        prepare(2 + side, 1, side)
    for side in range(2):
        build(0, side)

    def pairs(first_tile, count):
        for pair in range(count):
            parity, tile = pair % 2, first_tile + 2 * pair
            for side in range(2):
                add(tile + side, parity, side)
            for side in range(2):
                build(1 - parity, side)
            for side in range(2):
                prepare(tile + 4 + side, parity, side)

    long_steps = tile_total // (2 * LONG)

    def long_step(step, unused):
        pairs(2 * LONG * step, LONG)
        return unused

    def short_step(step, unused):
        pairs(2 * LONG * long_steps + 4 * step, 2)
        return unused

    lax.fori_loop(0, long_steps, long_step, 0)
    lax.fori_loop(0, (tile_total - 2 * LONG * long_steps + 3) // 4, short_step, 0)
    copy.wait()

    square_sum = jnp.float32(0.0)
    for device in range(groups * members):
        square_sum = square_sum + extra_ref[device, 0, 2 * layer_dev]
    scale = 1.0 / jnp.sqrt(jnp.full((1, wide), square_sum, jnp.float32))
    chunk = 16

    def screen(step, unused):
        at = pl.multiple_of(step * chunk, chunk)
        depth = depth_ref[pl.ds(at, chunk), :]
        total = jnp.zeros((chunk, wide), jnp.float32)
        for region in range(regions):
            layer_depth = extra_ref[region // layer_dev * members, 0, layer_dev + region % layer_dev]
            halves = (2.0 * layer_depth) * depth
            nearest = jnp.round(halves)
            cosine, sine = half_turn(halves - nearest)
            part = sum_ref[region, pl.ds(at, chunk), :wide] * cosine
            part = part - sum_ref[region, pl.ds(at, chunk), wide:] * sine
            total = total + jnp.where((nearest.astype(jnp.int32) & 1) == 1, -part, part)
        out_ref[pl.ds(at, chunk), :] = (total * scale)[:, :columns]
        return unused

    lax.fori_loop(0, rows // chunk, screen, 0)


def body(
    visibilities,
    weights,
    cell_index,
    kernel_index,
    layer_index,
    tile_counts,
    kernel_table,
    layer_depth,
):
    layer_dev = layer_depth.shape[0]
    groups, members = lax.axis_size("wa"), lax.axis_size("bl")
    tiles, samples = cell_index.shape[1:]
    slots = tiles * samples
    rows, columns = GRID // groups, GRID // members
    wide = max(columns, LANES)
    vmem = pl.BlockSpec(memory_space=pltpu.VMEM)
    smem = pl.BlockSpec(memory_space=pltpu.SMEM)
    devices = groups * members
    packed = pl.pallas_call(
        functools.partial(pack_kernel, layer_dev),
        out_shape=jax.ShapeDtypeStruct((devices, SENT, FIELDS // SENT * slots + LANES), jnp.float32),
        in_specs=[smem, smem, vmem, vmem, vmem, vmem, vmem],
        out_specs=vmem,
        name="pack_slots",
    )(
        tile_counts,
        layer_depth,
        visibilities.reshape(2 * tiles, samples),
        weights.reshape(tiles, samples),
        cell_index.reshape(tiles, samples),
        kernel_index.reshape(tiles, samples),
        layer_index.reshape(tiles, samples),
    )
    gathered = lax.all_to_all(packed, ("wa", "bl"), split_axis=0, concat_axis=0, tiled=True)
    period = min(rows, LANES)
    steps_u, steps_v = -(-period // 64) * 8, -(-wide // 64) * 8
    shapes = [(2, rows, LANES), (2, 8, LANES), (2, steps_u, LANES)]
    shapes = shapes + [(2, wide, LANES), (2, 8, LANES), (2, steps_v, LANES), (rows, wide)]
    tables = pl.pallas_call(
        table_kernel,
        out_shape=[jax.ShapeDtypeStruct(shape, jnp.float32) for shape in shapes],
        in_specs=[vmem],
        out_specs=[vmem] * len(shapes),
        compiler_params=pltpu.CompilerParams(vmem_limit_bytes=8 << 20),
        cost_estimate=pl.CostEstimate(flops=4000000, bytes_accessed=1000000, transcendentals=0),
        name="lane_tables",
    )(kernel_table.T)
    region_tiles = members * slots // LANES + 2 * (slots // LANES) + 1

    def four_of(shape, kind):
        return [[pltpu.VMEM(shape, kind) for side in range(2)] for parity in range(2)]

    return pl.pallas_call(
        functools.partial(image_kernel, layer_dev, groups, members),
        out_shape=jax.ShapeDtypeStruct((rows, columns), jnp.float32),
        in_specs=[vmem] * (1 + len(shapes)),
        out_specs=vmem,
        scratch_shapes=[
            pltpu.SMEM((devices, 1, LANES), jnp.float32),
            pltpu.VMEM((groups * layer_dev * region_tiles, FIELDS, LANES), jnp.float32),
            four_of((8, LANES), jnp.int32),
            four_of((2, 16 + steps_u + steps_v, LANES), jnp.float32),
            four_of((2, 2, rows, LANES), jnp.bfloat16),
            four_of((2, 2, 2 * wide, LANES), jnp.bfloat16),
            pltpu.VMEM((groups * layer_dev, rows, 2 * wide), jnp.float32),
            pltpu.SMEM((groups * layer_dev,), jnp.int32),
            pltpu.SMEM((groups * layer_dev,), jnp.int32),
            pltpu.SemaphoreType.DMA,
        ],
        compiler_params=pltpu.CompilerParams(vmem_limit_bytes=24 << 20),
        name="slots_to_image",
    )(gathered, *tables)


def solution(mesh):
    in_specs = (
        P("wa", "bl", None, None),
        P("wa", "bl", None),
        P("wa", "bl", None),
        P("wa", "bl", None),
        P("wa", "bl", None),
        P("wa", "bl"),
        P(),
        P("wa"),
    )
    return jax.shard_map(body, mesh=mesh, in_specs=in_specs, out_specs=P("wa", "bl"), check_vma=False)
```

profile of v0, /device:TPU:0, one launch (start us, length us, event | category | flops | bytes accessed | tf_op | source)
XLA Modules:
  0.0 29.0 jit_solution(10656456816211686337)
XLA Ops:
  0.0 1.8 %pack_slots.1 = f32[32,2,640]{2,1,0:T(2,128)} custom-call(s32[1,2]{1,0:T(1,128)} %count_ref.1, f32[2]{0:T(128)} %depth_ref.1, f32[4,128]{1,0:T(4,128)} %bitcast.7, f32[2,128]{1,0:T(2,128)} %bitcast.8, s32[2,128]{1,0:T(2,128)} %bitcast.9, s32[2,128]{1,0:T(2,128)} %bitcast.10, s32[2,128]{1,0:T(2,128)} %bitcast.11), custom_call_target="tpu_custom_call" | custom-call | tf_op jit(solution)/shard_map/pack_slots/pallas_call | solution.py:404
  1.8 0.0 copy-start
  1.8 7.3 %all-to-all-start = ((f32[32,2,640]{2,1,0:T(2,128)}), f32[32,2,640]{2,1,0:T(2,128)S(1)}, u32[]{:S(2)}, u32[]{:S(2)}) async-start(f32[32,2,640]{2,1,0:T(2,128)} %pack_slots.1), calls=%async_computation | async-start | bytes 327680 | tf_op jit(solution)/shard_map/all_to_all | solution.py:419
  9.2 0.0 copy-done
  9.2 0.7 %lane_tables.1 = (f32[2,256,128]{2,1,0:T(8,128)S(1)}, f32[2,8,128]{2,1,0:T(8,128)S(1)}, f32[2,16,128]{2,1,0:T(8,128)S(1)}, f32[2,128,128]{2,1,0:T(8,128)S(1)}, f...) custom-call(f32[8,16]{1,0:T(8,128)S(1)} %bitcast.6), custom_call_target="tpu_custom_call" | custom-call | flops 4000000 | bytes 1000000 | tf_op jit(solution)/shard_map/lane_tables/pallas_call | solution.py:424
  9.9 7.9 %all-to-all-done.slot_ref = f32[32,2,640]{2,1,0:T(2,128)S(1)} async-done(((f32[32,2,640]{2,1,0:T(2,128)}), f32[32,2,640]{2,1,0:T(2,128)S(1)}, u32[]{:S(2)}, u32[]{:S(2)}) %all-to-all-start) | async-done | bytes 163872 | tf_op jit(solution)/shard_map/all_to_all | solution.py:419
  17.8 11.2 %slots_to_image.1 = f32[256,128]{1,0:T(8,128)} custom-call(f32[32,2,640]{2,1,0:T(2,128)S(1)} %all-to-all-done.slot_ref, f32[2,256,128]{2,1,0:T(8,128)S(1)} %get-tuple-element.12.first_u, f32[2,8,128]{2,1,0:T(8,128)S(1)} %get-tuple-element.13.base_u, f32[2,16,128]{2,1,0:T(8,128)S(1)} %get-tuple-element.14.step_u, ...), custom_call_target="tpu_custom_call" | custom-call | tf_op jit(solution)/shard_map/slots_to_image/pallas_call | solution.py:438
Async XLA Ops:
  1.8 7.3 %copy-start = (f32[16,8]{0,1:T(8,128)S(1)}, f32[16,8]{0,1:T(8,128)}, u32[]{:S(2)}) copy-start(f32[16,8]{0,1:T(8,128)} %param.14) | copy-start | bytes 1540
  1.8 16.0 %all-to-all-start = ((f32[32,2,640]{2,1,0:T(2,128)}), f32[32,2,640]{2,1,0:T(2,128)S(1)}, u32[]{:S(2)}, u32[]{:S(2)}) async-start(f32[32,2,640]{2,1,0:T(2,128)} %pack_slots.1), calls=%async_computation | async-start | bytes 327680 | tf_op jit(solution)/shard_map/all_to_all | solution.py:419
where the time goes:
time: 29.2 us; the launch traced here: 29 us
  Pallas kernels  13.8 us (47%)
  waiting for transfers between devices  7.87 us (27%)
  starting transfers between devices  7.33 us (25%)
    pallas_call x1, Pallas kernels, body(): pl.pallas_call(functools.partial(image_kernel, layer_dev, groups, members...  11.2 us
    all_to_all x1, waiting for transfers between devices, body(): lax.all_to_all(packed, ('wa', 'bl'), split_axis=0, concat_axis=0, tiled=T...  7.87 us
    all_to_all x1, starting transfers between devices, body(): lax.all_to_all(packed, ('wa', 'bl'), split_axis=0, concat_axis=0, tiled=T...  7.33 us
    pallas_call x1, Pallas kernels, body(): pl.pallas_call(functools.partial(pack_kernel, layer_dev), out_shape=jax.S...  1.83 us
    pallas_call x1, Pallas kernels, body(): pl.pallas_call(table_kernel, out_shape=[jax.ShapeDtypeStruct(shape, jnp.f...  0.74 us
  transfers between devices with their start and end apart: 1, of which 1 were waited for; matrix products, arithmetic and copies ran while one was open for 0% of the time, Pallas kernels for 3%

commit v1 on v0

--- a/solution.py
+++ b/solution.py
@@ -17,7 +17,7 @@
 LOW = LANES // OVERSAMPLE
 FIELDS = 4
 LONG = 4
-SENT = 2
+SENT = 1
 
 highest = lax.Precision.HIGHEST
 last_dims = (((1,), (1,)), ((), ()))
@@ -50,6 +50,13 @@
     cosine, sine = half_turn(step.astype(jnp.float32) * (2.0 / GRID))
     flip = (moved & (GRID // 2)) != 0
     return jnp.where(flip, -cosine, cosine), jnp.where(flip, -sine, sine)
+
+
+def screens(layer_depth, depth):
+    halves = (2.0 * layer_depth) * depth
+    nearest = jnp.round(halves)
+    cosine, sine = half_turn(halves - nearest)
+    return cosine, sine, (nearest.astype(jnp.int32) & 1) == 1
 
 
 def split_two(value):
@@ -126,7 +133,7 @@
         out_ref[device, :, FIELDS // SENT * slots :] = extra
 
 
-def table_kernel(taps_ref, first_u, base_u, step_u, first_v, base_v, step_v, depth_ref):
+def table_kernel(taps_ref, layer_ref, first_u, base_u, step_u, first_v, base_v, step_v, depth_ref, screen_ref):
     rows, columns = depth_ref.shape
     row_start = lax.axis_index("wa") * rows
     column_start = lax.axis_index("bl") * (GRID // lax.axis_size("bl"))
@@ -157,7 +164,12 @@
     pixel_size = FIELD_OF_VIEW / GRID
     x_coord = (row_start + iota((rows, columns), 0) - GRID // 2).astype(jnp.float32) * pixel_size
     y_coord = (column_start + iota((rows, columns), 1) - GRID // 2).astype(jnp.float32) * pixel_size
-    depth_ref[...] = jnp.sqrt(jnp.maximum(1.0 - x_coord * x_coord - y_coord * y_coord, 0.0)) - 1.0
+    depth = jnp.sqrt(jnp.maximum(1.0 - x_coord * x_coord - y_coord * y_coord, 0.0)) - 1.0
+    depth_ref[...] = depth
+    for layer in range(screen_ref.shape[0]):
+        cosine, sine, odd = screens(layer_ref[layer], depth)
+        screen_ref[layer, 0] = jnp.where(odd, -cosine, cosine)
+        screen_ref[layer, 1] = jnp.where(odd, -sine, sine)
 
 
 def image_kernel(
@@ -172,6 +184,7 @@
     base_v,
     step_v,
     depth_ref,
+    screen_ref,
     out_ref,
     extra_ref,
     stream_ref,
@@ -362,20 +375,26 @@
     for device in range(groups * members):
         square_sum = square_sum + extra_ref[device, 0, 2 * layer_dev]
     scale = 1.0 / jnp.sqrt(jnp.full((1, wide), square_sum, jnp.float32))
-    chunk = 16
+    chunk = min(64, rows)
+    own_group = lax.axis_index("wa")
 
     def screen(step, unused):
         at = pl.multiple_of(step * chunk, chunk)
         depth = depth_ref[pl.ds(at, chunk), :]
         total = jnp.zeros((chunk, wide), jnp.float32)
-        for region in range(regions):
-            layer_depth = extra_ref[region // layer_dev * members, 0, layer_dev + region % layer_dev]
-            halves = (2.0 * layer_depth) * depth
-            nearest = jnp.round(halves)
-            cosine, sine = half_turn(halves - nearest)
-            part = sum_ref[region, pl.ds(at, chunk), :wide] * cosine
-            part = part - sum_ref[region, pl.ds(at, chunk), wide:] * sine
-            total = total + jnp.where((nearest.astype(jnp.int32) & 1) == 1, -part, part)
+        for turn_on in range(groups):
+            group = (own_group + turn_on) % groups
+            for layer in range(layer_dev):
+                region = group * layer_dev + layer
+                real = sum_ref[region, pl.ds(at, chunk), :wide]
+                imag = sum_ref[region, pl.ds(at, chunk), wide:]
+                if turn_on == 0:
+                    total = total + real * screen_ref[layer, 0, pl.ds(at, chunk)]
+                    total = total - imag * screen_ref[layer, 1, pl.ds(at, chunk)]
+                else:
+                    cosine, sine, odd = screens(extra_ref[group * members, 0, layer_dev + layer], depth)
+                    part = real * cosine - imag * sine
+                    total = total + jnp.where(odd, -part, part)
         out_ref[pl.ds(at, chunk), :] = (total * scale)[:, :columns]
         return unused
 
@@ -421,15 +440,16 @@
     steps_u, steps_v = -(-period // 64) * 8, -(-wide // 64) * 8
     shapes = [(2, rows, LANES), (2, 8, LANES), (2, steps_u, LANES)]
     shapes = shapes + [(2, wide, LANES), (2, 8, LANES), (2, steps_v, LANES), (rows, wide)]
+    shapes = shapes + [(layer_dev, 2, rows, wide)]
     tables = pl.pallas_call(
         table_kernel,
         out_shape=[jax.ShapeDtypeStruct(shape, jnp.float32) for shape in shapes],
-        in_specs=[vmem],
+        in_specs=[vmem, smem],
         out_specs=[vmem] * len(shapes),
         compiler_params=pltpu.CompilerParams(vmem_limit_bytes=8 << 20),
         cost_estimate=pl.CostEstimate(flops=4000000, bytes_accessed=1000000, transcendentals=0),
         name="lane_tables",
-    )(kernel_table.T)
+    )(kernel_table.T, layer_depth)
     region_tiles = members * slots // LANES + 2 * (slots // LANES) + 1
 
     def four_of(shape, kind):

time: 29.2 us -> 27.9 us (0.955)
  waiting for transfers between devices: 7.87 us -> 6.24 us
  local copies, waits for them, and re-layouts: 0.01 us -> 0.64 us
  Pallas kernels: 13.8 us -> 13.4 us
    all_to_all x1, waiting for transfers between devices: 7.87 us -> 6.24 us  [body(): lax.all_to_all(packed, ('wa', 'bl'), split_axis=0, concat_axis=0, tiled=T...]
    pallas_call x1, Pallas kernels: 11.2 us -> 10 us  [body(): pl.pallas_call(functools.partial(image_kernel, layer_dev, groups, members...]
    pallas_call x1, Pallas kernels: 0.74 us -> 1.5 us  [body(): pl.pallas_call(table_kernel, out_shape=[jax.ShapeDtypeStruct(shape, jnp.f...]
    unnamed x2 -> x4, local copies, waits for them, and re-layouts: 0.01 us -> 0.64 us
  transfers between devices with their start and end apart: 1 -> 1, of which waited for: 1 -> 1; matrix products, arithmetic and copies ran while one was open for 0% -> 0% of each run, Pallas kernels for 3% -> 5%
where the time goes in v1:
time: 27.9 us; the launch traced here: 27.6 us
  Pallas kernels  13.4 us (48%)
  starting transfers between devices  7.33 us (26%)
  waiting for transfers between devices  6.24 us (22%)
  local copies, waits for them, and re-layouts  0.64 us (2%)
    pallas_call x1, Pallas kernels, body(): pl.pallas_call(functools.partial(image_kernel, layer_dev, groups, members...  10 us
    all_to_all x1, starting transfers between devices, body(): lax.all_to_all(packed, ('wa', 'bl'), split_axis=0, concat_axis=0, tiled=T...  7.33 us
    all_to_all x1, waiting for transfers between devices, body(): lax.all_to_all(packed, ('wa', 'bl'), split_axis=0, concat_axis=0, tiled=T...  6.24 us
    pallas_call x1, Pallas kernels, body(): pl.pallas_call(functools.partial(pack_kernel, layer_dev), out_shape=jax.S...  1.85 us
    pallas_call x1, Pallas kernels, body(): pl.pallas_call(table_kernel, out_shape=[jax.ShapeDtypeStruct(shape, jnp.f...  1.5 us
    unnamed x4, local copies, waits for them, and re-layouts  0.64 us
  transfers between devices with their start and end apart: 1, of which 1 were waited for; matrix products, arithmetic and copies ran while one was open for 0% of the time, Pallas kernels for 5%

profile of v1, /device:TPU:0, one launch (start us, length us, event | category | flops | bytes accessed | tf_op | source)
XLA Modules:
  0.0 27.6 jit_solution(12051461250090065066)
XLA Ops:
  0.0 1.8 %pack_slots.1 = f32[32,1,1152]{2,1,0:T(1,128)} custom-call(s32[1,2]{1,0:T(1,128)} %count_ref.1, f32[2]{0:T(128)} %layer_ref.1, f32[4,128]{1,0:T(4,128)} %bitcast.7, f32[2,128]{1,0:T(2,128)} %bitcast.8, s32[2,128]{1,0:T(2,128)} %bitcast.9, s32[2,128]{1,0:T(2,128)} %bitcast.10, s32[2,128]{1,0:T(2,128)} %bitcast.11), custom_call_target="tpu_custom_call" | custom-call | tf_op jit(solution)/shard_map/pack_slots/pallas_call | solution.py:423
  1.8 0.0 copy-start.1
  1.8 7.3 %all-to-all-start = ((f32[32,1,1152]{2,1,0:T(1,128)}), f32[32,1,1152]{2,1,0:T(1,128)S(1)}, u32[]{:S(2)}, u32[]{:S(2)}) async-start(f32[32,1,1152]{2,1,0:T(1,128)} %pack_slots.1), calls=%async_computation | async-start | bytes 294912 | tf_op jit(solution)/shard_map/all_to_all | solution.py:438
  9.2 0.0 copy-start
  9.2 0.0 copy-done.1
  9.2 0.6 %copy-done = f32[2]{0:T(128)S(1)} copy-done((f32[2]{0:T(128)S(1)}, f32[2]{0:T(128)}, u32[]{:S(2)}) %copy-start) | copy-done | bytes 32
  9.8 1.5 %lane_tables.1 = (f32[2,256,128]{2,1,0:T(8,128)S(1)}, f32[2,8,128]{2,1,0:T(8,128)S(1)}, f32[2,16,128]{2,1,0:T(8,128)S(1)}, f32[2,128,128]{2,1,0:T(8,128)S(1)}, f...) custom-call(f32[8,16]{1,0:T(8,128)S(1)} %bitcast.6, ...), custom_call_target="tpu_custom_call" | custom-call | flops 4000000 | bytes 1000000 | tf_op jit(solution)/shard_map/lane_tables/pallas_call | solution.py:444
  11.4 6.2 %all-to-all-done.slot_ref = f32[32,1,1152]{2,1,0:T(1,128)S(1)} async-done(((f32[32,1,1152]{2,1,0:T(1,128)}), f32[32,1,1152]{2,1,0:T(1,128)S(1)}, u32[]{:S(2)}, u32[]{:S(2)}) %all-to-all-start) | async-done | bytes 147488 | tf_op jit(solution)/shard_map/all_to_all | solution.py:438
  17.6 10.0 %slots_to_image.1 = f32[256,128]{1,0:T(8,128)} custom-call(f32[32,1,1152]{2,1,0:T(1,128)S(1)} %all-to-all-done.slot_ref, f32[2,256,128]{2,1,0:T(8,128)S(1)} %get-tuple-element.13.first_u, f32[2,8,128]{2,1,0:T(8,128)S(1)} %get-tuple-element.14.base_u, f32[2,16,128]{2,1,0:T(8,128)S(1)} %get-tuple-element.15.step_u, ...), custom_call_target="tpu_custom_call" | custom-call | tf_op jit(solution)/shard_map/slots_to_image/pallas_call | solution.py:458
Async XLA Ops:
  1.8 7.3 %copy-start.1 = (f32[16,8]{0,1:T(8,128)S(1)}, f32[16,8]{0,1:T(8,128)}, u32[]{:S(2)}) copy-start(f32[16,8]{0,1:T(8,128)} %param.14) | copy-start | bytes 1540
  1.8 15.7 %all-to-all-start = ((f32[32,1,1152]{2,1,0:T(1,128)}), f32[32,1,1152]{2,1,0:T(1,128)S(1)}, u32[]{:S(2)}, u32[]{:S(2)}) async-start(f32[32,1,1152]{2,1,0:T(1,128)} %pack_slots.1), calls=%async_computation | async-start | bytes 294912 | tf_op jit(solution)/shard_map/all_to_all | solution.py:438
  9.2 0.7 %copy-start = (f32[2]{0:T(128)S(1)}, f32[2]{0:T(128)}, u32[]{:S(2)}) copy-start(f32[2]{0:T(128)} %layer_ref.1) | copy-start | bytes 28

commit v2 on v1

--- a/solution.py
+++ b/solution.py
@@ -368,7 +368,15 @@
         return unused
 
     lax.fori_loop(0, long_steps, long_step, 0)
-    lax.fori_loop(0, (tile_total - 2 * LONG * long_steps + 3) // 4, short_step, 0)
+    rest = tile_total - 2 * LONG * long_steps
+    short_steps = (rest + 1) // 4
+    lax.fori_loop(0, short_steps, short_step, 0)
+
+    @pl.when(rest > 4 * short_steps)
+    def last_pair():
+        for side in range(2):
+            add(2 * LONG * long_steps + 4 * short_steps + side, 0, side)
+
     copy.wait()
 
     square_sum = jnp.float32(0.0)

time: 27.9 us -> 28.4 us (1.018)
  Pallas kernels: 13.4 us -> 13.9 us
    pallas_call x1, Pallas kernels: 10 us -> 10.6 us  [body(): pl.pallas_call(functools.partial(image_kernel, layer_dev, groups, members...]
where the time goes in v2:
time: 28.4 us; the launch traced here: 28.1 us
  Pallas kernels  13.9 us (49%)
  starting transfers between devices  7.33 us (26%)
  waiting for transfers between devices  6.24 us (22%)
  local copies, waits for them, and re-layouts  0.64 us (2%)
    pallas_call x1, Pallas kernels, body(): pl.pallas_call(functools.partial(image_kernel, layer_dev, groups, members...  10.6 us
    all_to_all x1, starting transfers between devices, body(): lax.all_to_all(packed, ('wa', 'bl'), split_axis=0, concat_axis=0, tiled=T...  7.33 us
    all_to_all x1, waiting for transfers between devices, body(): lax.all_to_all(packed, ('wa', 'bl'), split_axis=0, concat_axis=0, tiled=T...  6.24 us
    pallas_call x1, Pallas kernels, body(): pl.pallas_call(functools.partial(pack_kernel, layer_dev), out_shape=jax.S...  1.85 us
    pallas_call x1, Pallas kernels, body(): pl.pallas_call(table_kernel, out_shape=[jax.ShapeDtypeStruct(shape, jnp.f...  1.5 us
    unnamed x4, local copies, waits for them, and re-layouts  0.64 us
  transfers between devices with their start and end apart: 1, of which 1 were waited for; matrix products, arithmetic and copies ran while one was open for 0% of the time, Pallas kernels for 5%

profile of v2, /device:TPU:0, one launch (start us, length us, event | category | flops | bytes accessed | tf_op | source)
XLA Modules:
  0.0 28.1 jit_solution(1778102362933513356)
XLA Ops:
  0.0 1.8 %pack_slots.1 = f32[32,1,1152]{2,1,0:T(1,128)} custom-call(s32[1,2]{1,0:T(1,128)} %count_ref.1, f32[2]{0:T(128)} %layer_ref.1, f32[4,128]{1,0:T(4,128)} %bitcast.7, f32[2,128]{1,0:T(2,128)} %bitcast.8, s32[2,128]{1,0:T(2,128)} %bitcast.9, s32[2,128]{1,0:T(2,128)} %bitcast.10, s32[2,128]{1,0:T(2,128)} %bitcast.11), custom_call_target="tpu_custom_call" | custom-call | tf_op jit(solution)/shard_map/pack_slots/pallas_call | solution.py:431
  1.8 0.0 copy-start.1
  1.8 7.3 %all-to-all-start = ((f32[32,1,1152]{2,1,0:T(1,128)}), f32[32,1,1152]{2,1,0:T(1,128)S(1)}, u32[]{:S(2)}, u32[]{:S(2)}) async-start(f32[32,1,1152]{2,1,0:T(1,128)} %pack_slots.1), calls=%async_computation | async-start | bytes 294912 | tf_op jit(solution)/shard_map/all_to_all | solution.py:446
  9.2 0.0 copy-start
  9.2 0.0 copy-done.1
  9.2 0.6 %copy-done = f32[2]{0:T(128)S(1)} copy-done((f32[2]{0:T(128)S(1)}, f32[2]{0:T(128)}, u32[]{:S(2)}) %copy-start) | copy-done | bytes 32
  9.8 1.5 %lane_tables.1 = (f32[2,256,128]{2,1,0:T(8,128)S(1)}, f32[2,8,128]{2,1,0:T(8,128)S(1)}, f32[2,16,128]{2,1,0:T(8,128)S(1)}, f32[2,128,128]{2,1,0:T(8,128)S(1)}, f...) custom-call(f32[8,16]{1,0:T(8,128)S(1)} %bitcast.6, ...), custom_call_target="tpu_custom_call" | custom-call | flops 4000000 | bytes 1000000 | tf_op jit(solution)/shard_map/lane_tables/pallas_call | solution.py:452
  11.4 6.2 %all-to-all-done.slot_ref = f32[32,1,1152]{2,1,0:T(1,128)S(1)} async-done(((f32[32,1,1152]{2,1,0:T(1,128)}), f32[32,1,1152]{2,1,0:T(1,128)S(1)}, u32[]{:S(2)}, u32[]{:S(2)}) %all-to-all-start) | async-done | bytes 147488 | tf_op jit(solution)/shard_map/all_to_all | solution.py:446
  17.6 10.6 %slots_to_image.1 = f32[256,128]{1,0:T(8,128)} custom-call(f32[32,1,1152]{2,1,0:T(1,128)S(1)} %all-to-all-done.slot_ref, f32[2,256,128]{2,1,0:T(8,128)S(1)} %get-tuple-element.13.first_u, f32[2,8,128]{2,1,0:T(8,128)S(1)} %get-tuple-element.14.base_u, f32[2,16,128]{2,1,0:T(8,128)S(1)} %get-tuple-element.15.step_u, ...), custom_call_target="tpu_custom_call" | custom-call | tf_op jit(solution)/shard_map/slots_to_image/pallas_call | solution.py:466
Async XLA Ops:
  1.8 7.3 %copy-start.1 = (f32[16,8]{0,1:T(8,128)S(1)}, f32[16,8]{0,1:T(8,128)}, u32[]{:S(2)}) copy-start(f32[16,8]{0,1:T(8,128)} %param.14) | copy-start | bytes 1540
  1.8 15.7 %all-to-all-start = ((f32[32,1,1152]{2,1,0:T(1,128)}), f32[32,1,1152]{2,1,0:T(1,128)S(1)}, u32[]{:S(2)}, u32[]{:S(2)}) async-start(f32[32,1,1152]{2,1,0:T(1,128)} %pack_slots.1), calls=%async_computation | async-start | bytes 294912 | tf_op jit(solution)/shard_map/all_to_all | solution.py:446
  9.2 0.7 %copy-start = (f32[2]{0:T(128)S(1)}, f32[2]{0:T(128)}, u32[]{:S(2)}) copy-start(f32[2]{0:T(128)} %layer_ref.1) | copy-start | bytes 28

commit v3 on v2

--- a/solution.py
+++ b/solution.py
@@ -383,7 +383,7 @@
     for device in range(groups * members):
         square_sum = square_sum + extra_ref[device, 0, 2 * layer_dev]
     scale = 1.0 / jnp.sqrt(jnp.full((1, wide), square_sum, jnp.float32))
-    chunk = min(64, rows)
+    chunk = min(128, rows)
     own_group = lax.axis_index("wa")
 
     def screen(step, unused):

time: 28.4 us -> 27.6 us (0.972)
  Pallas kernels: 13.9 us -> 13 us
    pallas_call x1, Pallas kernels: 10.6 us -> 9.67 us  [body(): pl.pallas_call(functools.partial(image_kernel, layer_dev, groups, members...]
  transfers between devices with their start and end apart: 1 -> 1, of which waited for: 1 -> 1; matrix products, arithmetic and copies ran while one was open for 0% -> 0% of each run, Pallas kernels for 5% -> 6%
where the time goes in v3:
time: 27.6 us; the launch traced here: 27.3 us
  Pallas kernels  13 us (47%)
  starting transfers between devices  7.33 us (27%)
  waiting for transfers between devices  6.24 us (23%)
  local copies, waits for them, and re-layouts  0.64 us (2%)
    pallas_call x1, Pallas kernels, body(): pl.pallas_call(functools.partial(image_kernel, layer_dev, groups, members...  9.67 us
    all_to_all x1, starting transfers between devices, body(): lax.all_to_all(packed, ('wa', 'bl'), split_axis=0, concat_axis=0, tiled=T...  7.33 us
    all_to_all x1, waiting for transfers between devices, body(): lax.all_to_all(packed, ('wa', 'bl'), split_axis=0, concat_axis=0, tiled=T...  6.24 us
    pallas_call x1, Pallas kernels, body(): pl.pallas_call(functools.partial(pack_kernel, layer_dev), out_shape=jax.S...  1.85 us
    pallas_call x1, Pallas kernels, body(): pl.pallas_call(table_kernel, out_shape=[jax.ShapeDtypeStruct(shape, jnp.f...  1.5 us
    unnamed x4, local copies, waits for them, and re-layouts  0.64 us
  transfers between devices with their start and end apart: 1, of which 1 were waited for; matrix products, arithmetic and copies ran while one was open for 0% of the time, Pallas kernels for 6%

profile of v3, /device:TPU:0, one launch (start us, length us, event | category | flops | bytes accessed | tf_op | source)
XLA Modules:
  0.0 27.3 jit_solution(4877155719027861881)
XLA Ops:
  0.0 1.8 %pack_slots.1 = f32[32,1,1152]{2,1,0:T(1,128)} custom-call(s32[1,2]{1,0:T(1,128)} %count_ref.1, f32[2]{0:T(128)} %layer_ref.1, f32[4,128]{1,0:T(4,128)} %bitcast.7, f32[2,128]{1,0:T(2,128)} %bitcast.8, s32[2,128]{1,0:T(2,128)} %bitcast.9, s32[2,128]{1,0:T(2,128)} %bitcast.10, s32[2,128]{1,0:T(2,128)} %bitcast.11), custom_call_target="tpu_custom_call" | custom-call | tf_op jit(solution)/shard_map/pack_slots/pallas_call | solution.py:431
  1.8 0.0 copy-start.1
  1.8 7.3 %all-to-all-start = ((f32[32,1,1152]{2,1,0:T(1,128)}), f32[32,1,1152]{2,1,0:T(1,128)S(1)}, u32[]{:S(2)}, u32[]{:S(2)}) async-start(f32[32,1,1152]{2,1,0:T(1,128)} %pack_slots.1), calls=%async_computation | async-start | bytes 294912 | tf_op jit(solution)/shard_map/all_to_all | solution.py:446
  9.2 0.0 copy-start
  9.2 0.0 copy-done.1
  9.2 0.6 %copy-done = f32[2]{0:T(128)S(1)} copy-done((f32[2]{0:T(128)S(1)}, f32[2]{0:T(128)}, u32[]{:S(2)}) %copy-start) | copy-done | bytes 32
  9.8 1.5 %lane_tables.1 = (f32[2,256,128]{2,1,0:T(8,128)S(1)}, f32[2,8,128]{2,1,0:T(8,128)S(1)}, f32[2,16,128]{2,1,0:T(8,128)S(1)}, f32[2,128,128]{2,1,0:T(8,128)S(1)}, f...) custom-call(f32[8,16]{1,0:T(8,128)S(1)} %bitcast.6, ...), custom_call_target="tpu_custom_call" | custom-call | flops 4000000 | bytes 1000000 | tf_op jit(solution)/shard_map/lane_tables/pallas_call | solution.py:452
  11.4 6.2 %all-to-all-done.slot_ref = f32[32,1,1152]{2,1,0:T(1,128)S(1)} async-done(((f32[32,1,1152]{2,1,0:T(1,128)}), f32[32,1,1152]{2,1,0:T(1,128)S(1)}, u32[]{:S(2)}, u32[]{:S(2)}) %all-to-all-start) | async-done | bytes 147488 | tf_op jit(solution)/shard_map/all_to_all | solution.py:446
  17.6 9.7 %slots_to_image.1 = f32[256,128]{1,0:T(8,128)} custom-call(f32[32,1,1152]{2,1,0:T(1,128)S(1)} %all-to-all-done.slot_ref, f32[2,256,128]{2,1,0:T(8,128)S(1)} %get-tuple-element.13.first_u, f32[2,8,128]{2,1,0:T(8,128)S(1)} %get-tuple-element.14.base_u, f32[2,16,128]{2,1,0:T(8,128)S(1)} %get-tuple-element.15.step_u, ...), custom_call_target="tpu_custom_call" | custom-call | tf_op jit(solution)/shard_map/slots_to_image/pallas_call | solution.py:466
Async XLA Ops:
  1.8 7.3 %copy-start.1 = (f32[16,8]{0,1:T(8,128)S(1)}, f32[16,8]{0,1:T(8,128)}, u32[]{:S(2)}) copy-start(f32[16,8]{0,1:T(8,128)} %param.14) | copy-start | bytes 1540
  1.8 15.7 %all-to-all-start = ((f32[32,1,1152]{2,1,0:T(1,128)}), f32[32,1,1152]{2,1,0:T(1,128)S(1)}, u32[]{:S(2)}, u32[]{:S(2)}) async-start(f32[32,1,1152]{2,1,0:T(1,128)} %pack_slots.1), calls=%async_computation | async-start | bytes 294912 | tf_op jit(solution)/shard_map/all_to_all | solution.py:446
  9.2 0.7 %copy-start = (f32[2]{0:T(128)S(1)}, f32[2]{0:T(128)}, u32[]{:S(2)}) copy-start(f32[2]{0:T(128)} %layer_ref.1) | copy-start | bytes 28
